TPU v7x, 32 devices: a whole 2x2x4 slice. The times are simulated.
32 devices in a mesh: heads: 2 (over x), seq: 16 (over z, y, core).
Axes of the slice: x: 2, y: 2, z: 4, core: 2. Of those that a mesh axis runs over, the one named last changes fastest.
Arguments:
- query_nope: bfloat16 [1, 4, 128, 128], P(None, None, 'heads'), may hold values from -6 to 6
- query_rope: bfloat16 [1, 4, 128, 64], P(None, None, 'heads'), may hold values from -8 to 8
- latent_cache: bfloat16 [1, 8192, 512], P(None, 'seq'), may hold values from -6 to 6
- rope_keys: bfloat16 [1, 64, 8192], P(None, None, 'seq'), may hold values from -8 to 8
- lengths: int32 [1], replicated, may hold values from 2 to 8189, as said below
- key_quant: bfloat16 [128, 512, 128], P('heads', 'seq'), may hold values from -127 to 127, as said below
- key_scale: float32 [128, 4], P('heads'), may hold values from 0.0006 to 0.0024
- value_quant: bfloat16 [128, 512, 128], P('heads', 'seq'), may hold values from -127 to 127, as said below
- value_scale: float32 [128, 4], P('heads'), may hold values from 0.0003 to 0.0012
- out_weight: bfloat16 [16384, 7168], P('heads', 'seq'), may hold values from -0.375 to 0.375
Outputs:
- attn_out: bfloat16 [1, 4, 7168], P(None, None, 'seq')
Inputs may be any that keep to these rules, and one draw needn't show every extreme that they name: `key_quant`: whole numbers. `value_quant`: whole numbers. `lengths`: one sequence has the largest allowed length, so that its last draft token sees all 8192 positions.
All inputs are finite; a program needn't handle non-finite values.
Results may differ from a plain program's by a relative error of at most 0.019.
Values may be sent and summed in bfloat16 or wider, within the bound.
A program may use at most 64 MiB of HBM per device.

v0:
```python
import functools

import jax
import jax.numpy as jnp
from jax import lax
from jax.experimental import pallas as pl
from jax.experimental.pallas import tpu as pltpu
from jax.sharding import PartitionSpec as P

QB = 128
MESH = pl.DeviceIdType.MESH
neg_large = -1e30
F32 = jnp.float32
BF16 = jnp.bfloat16


def scale_row(scale_ref, block, rows, heads):
    scales = scale_ref[...]
    line = jnp.sum(
        jnp.where(lax.broadcasted_iota(jnp.int32, scales.shape, 0) == block, scales, 0.0),
        axis=0,
        keepdims=True,
    )
    square = (heads, heads)
    diagonal = lax.broadcasted_iota(jnp.int32, square, 0) == lax.broadcasted_iota(jnp.int32, square, 1)
    column = jnp.sum(jnp.where(diagonal, line, 0.0), axis=1, keepdims=True)
    lane_head = lax.broadcasted_iota(jnp.int32, (heads, rows), 1) % heads
    own_head = lax.broadcasted_iota(jnp.int32, (heads, rows), 0)
    return jnp.sum(jnp.where(lane_head == own_head, column, 0.0), axis=0, keepdims=True)


def kernel(
    n,
    groups,
    heads,
    drafts,
    q_hbm,
    qr_hbm,
    cache_hbm,
    rope_hbm,
    len_ref,
    kq_hbm,
    ks_ref,
    vq_hbm,
    vs_ref,
    w_hbm,
    out_ref,
    q,
    qr,
    cache,
    rope,
    kq,
    vq,
    w,
    cache_t,
    vq_t,
    base,
    lat_all,
    stats,
    out_send,
    out_recv,
    part_send,
    part_recv,
    share_all,
    flat,
    heads_out,
    final,
    in_sem,
    lat_send,
    lat_recv,
    pass_send,
    st_send,
    st_recv,
    o_send,
    o_recv,
    p_send,
    p_recv,
    s_send,
    s_recv,
    f_send,
    f_recv,
):
    me = lax.axis_index("seq")
    group = lax.axis_index("heads")
    rows = q.shape[0]
    cols = lat_all.shape[1]
    width = vq.shape[1]
    positions = cache.shape[0]
    factor = (q.shape[1] + qr.shape[1]) ** (-0.5)

    loads = []
    for i, (src, dst) in enumerate(
        ((kq_hbm, kq), (q_hbm, q), (qr_hbm, qr), (rope_hbm, rope), (cache_hbm, cache), (vq_hbm, vq), (w_hbm, w))
    ):
        copy = pltpu.make_async_copy(src, dst, in_sem.at[i])
        if dst is not w:
            copy.start()
        loads.append(copy)
    kq_load, q_load, qr_load, rope_load, cache_load, vq_load, w_load = loads

    barrier = pltpu.get_barrier_semaphore()

    def greet_seq(j, c):
        pl.semaphore_signal(barrier, inc=1, device_id=(group, lax.rem(me + j, n)), device_id_type=MESH)
        return c

    def greet_heads(j, c):
        pl.semaphore_signal(barrier, inc=1, device_id=(lax.rem(group + j, groups), me), device_id_type=MESH)
        return c

    lax.fori_loop(1, n, greet_seq, 0)
    lax.fori_loop(1, groups, greet_heads, 0)

    def spread(src_of, dst, send, recv):
        def make(j):
            peer = lax.rem(me + j, n)
            return pltpu.make_async_remote_copy(
                src_ref=src_of(peer),
                dst_ref=dst.at[me],
                send_sem=send.at[peer],
                recv_sem=recv.at[me],
                device_id=(group, peer),
                device_id_type=MESH,
            )

        def go(j, c):
            make(j).start()
            return c

        lax.fori_loop(1, n, go, 0)

    def arrive(src_of, dst, send, recv):
        def wait(j, c):
            peer = lax.rem(me + j, n)
            pltpu.make_async_remote_copy(
                src_ref=src_of(peer),
                dst_ref=dst.at[peer],
                send_sem=send.at[peer],
                recv_sem=recv.at[peer],
                device_id=(group, peer),
                device_id_type=MESH,
            ).wait_recv()
            return c

        lax.fori_loop(1, n, wait, 0)

    def drain(src_of, dst, send, recv):
        def wait(j, c):
            peer = lax.rem(me + j, n)
            pltpu.make_async_remote_copy(
                src_ref=src_of(peer),
                dst_ref=dst.at[me],
                send_sem=send.at[peer],
                recv_sem=recv.at[me],
                device_id=(group, peer),
                device_id_type=MESH,
            ).wait_send()
            return c

        lax.fori_loop(1, n, wait, 0)

    block = (me * cols) // QB
    lane_head = lax.broadcasted_iota(jnp.int32, (1, rows), 1) % heads
    key_row = scale_row(ks_ref, block, rows, heads)
    value_row = scale_row(vs_ref, block, rows, heads)

    kq_load.wait()
    q_load.wait()
    every = lax.dot_general(kq[...], q[...], (((1,), (1,)), ((), ())), preferred_element_type=F32)
    every = every.reshape(heads, cols, rows)
    own = lax.broadcasted_iota(jnp.int32, (heads, 1, rows), 0) == lane_head[None]
    piece = jnp.sum(jnp.where(own, every, 0.0), axis=0) * key_row
    lat_all[me] = piece.astype(BF16)

    pl.semaphore_wait(barrier, n - 1 + groups - 1)

    partner = me + 1 - 2 * lax.rem(me, 2)

    def lat_copy(slot, peer, send):
        return pltpu.make_async_remote_copy(
            src_ref=lat_all.at[slot],
            dst_ref=lat_all.at[slot],
            send_sem=send,
            recv_sem=lat_recv.at[slot],
            device_id=(group, peer),
            device_id_type=MESH,
        )

    def like(j):
        return lax.rem(me + 2 * j, n)

    def lat_go(j, c):
        lat_copy(me, like(j), lat_send.at[like(j)]).start()
        return c

    def lat_pass(j, c):
        lat_copy(like(j), partner, pass_send.at[like(j)]).wait_recv()
        lat_copy(like(j), partner, pass_send.at[like(j)]).start()
        return c

    def lat_rest(j, c):
        other = lax.rem(partner + 2 * j, n)
        lat_copy(other, partner, pass_send.at[other]).wait_recv()
        return c

    def lat_drain(j, c):
        lat_copy(me, like(j), lat_send.at[like(j)]).wait_send()
        lat_copy(like(j), partner, pass_send.at[like(j)]).wait_send()
        return c

    lax.fori_loop(1, n // 2, lat_go, 0)
    lat_copy(me, partner, lat_send.at[partner]).start()
    w_load.start()

    qr_load.wait()
    rope_load.wait()
    base[...] = lax.dot_general(
        rope[...].T, qr[...], (((1,), (1,)), ((), ())), preferred_element_type=F32
    )
    cache_load.wait()
    cache_t[...] = cache[...].T
    lax.fori_loop(1, n // 2, lat_pass, 0)
    position = me * positions + lax.broadcasted_iota(jnp.int32, (positions, rows), 0)
    horizon = len_ref[0] + lax.broadcasted_iota(jnp.int32, (positions, rows), 1) // heads
    visible = position < horizon

    lax.fori_loop(0, n // 2, lat_rest, 0)
    query_latent = lat_all[...].reshape(n * cols, rows)
    scores = (jnp.dot(cache[...], query_latent, preferred_element_type=F32) + base[...]) * factor
    block_max = jnp.max(jnp.where(visible, scores, neg_large), axis=0, keepdims=True)
    probs = jnp.where(visible, jnp.exp(scores - block_max), 0.0)
    block_sum = jnp.sum(probs, axis=0, keepdims=True)
    stats[me, 0:1, :] = block_max
    stats[me, 1:2, :] = block_sum
    st = (lambda peer: stats.at[me], stats, st_send, st_recv)
    spread(*st)
    block_out = jnp.dot(cache_t[...], probs.astype(BF16), preferred_element_type=F32)
    out_send[...] = block_out.astype(BF16).reshape(n, cols, rows)
    o = (lambda peer: out_send.at[peer], out_recv, o_send, o_recv)
    spread(*o)
    out_recv[me] = out_send[me]
    vq_load.wait()
    vq_t[...] = vq[...].T

    arrive(*st)
    all_max = stats[:, 0:1, :]
    top = jnp.max(all_max, axis=0, keepdims=True)
    weight = jnp.exp(all_max - top)
    total = jnp.sum(weight * stats[:, 1:2, :], axis=0)
    arrive(*o)
    merged = jnp.sum(out_recv[...].astype(F32) * weight, axis=0) / total
    latent = jnp.where(own, merged[None], 0.0).astype(BF16).reshape(heads * cols, rows)
    partial = jnp.dot(vq_t[...], latent, preferred_element_type=F32) * value_row
    step = width // n
    for d in range(n):
        part_send[d] = partial[d * step : (d + 1) * step].astype(part_send.dtype)
    p = (lambda peer: part_send.at[peer], part_recv, p_send, p_recv)
    spread(*p)
    part_recv[me] = part_send[me]
    arrive(*p)
    share_all[me] = jnp.sum(part_recv[...].astype(F32), axis=0).astype(BF16)
    s = (lambda peer: share_all.at[me], share_all, s_send, s_recv)
    spread(*s)
    arrive(*s)
    head_t = jnp.concatenate([share_all[d].astype(F32) for d in range(n)], axis=0)
    heads_out[...] = head_t.T.reshape(drafts, heads, width)
    for k in range(heads):
        flat[:, k * width : (k + 1) * width] = heads_out[:, k, :].astype(BF16)
    w_load.wait()
    final[group] = lax.dot_general(
        flat[...], w[...], (((1,), (1,)), ((), ())), preferred_element_type=F32
    )

    def pair(j, at):
        peer = lax.rem(group + j, groups)
        return pltpu.make_async_remote_copy(
            src_ref=final.at[group],
            dst_ref=final.at[group if at else peer],
            send_sem=f_send.at[peer],
            recv_sem=f_recv.at[group if at else peer],
            device_id=(peer, me),
            device_id_type=MESH,
        )

    for j in range(1, groups):
        pair(j, True).start()
    for j in range(1, groups):
        pair(j, False).wait_recv()
    out_ref[...] = jnp.sum(final[...], axis=0).astype(BF16)
    for each in (st, o, p, s):
        drain(*each)
    lax.fori_loop(1, n // 2, lat_drain, 0)
    lat_copy(me, partner, lat_send.at[partner]).wait_send()
    for j in range(1, groups):
        pair(j, True).wait_send()


def solution(mesh):
    n = mesh.shape["seq"]
    groups = mesh.shape["heads"]

    def per_device(
        query_nope,
        query_rope,
        latent_cache,
        rope_keys,
        lengths,
        key_quant,
        key_scale,
        value_quant,
        value_scale,
        out_weight,
    ):
        batch, drafts, heads, nope = query_nope.shape
        rows = batch * drafts * heads
        rope = query_rope.shape[-1]
        positions, latent = latent_cache.shape[1:]
        cols = key_quant.shape[1]
        width = value_quant.shape[2]
        model = out_weight.shape[1]
        hbm = pl.BlockSpec(memory_space=pltpu.HBM)
        vmem = pl.BlockSpec(memory_space=pltpu.VMEM)
        smem = pl.BlockSpec(memory_space=pltpu.SMEM)
        dma = pltpu.SemaphoreType.DMA
        result = pl.pallas_call(
            functools.partial(kernel, n, groups, heads, drafts),
            out_shape=jax.ShapeDtypeStruct((drafts, model), BF16),
            in_specs=[hbm, hbm, hbm, hbm, smem, hbm, vmem, hbm, vmem, hbm],
            out_specs=vmem,
            scratch_shapes=[
                pltpu.VMEM((rows, nope), BF16),
                pltpu.VMEM((rows, rope), BF16),
                pltpu.VMEM((positions, latent), BF16),
                pltpu.VMEM((rope, positions), BF16),
                pltpu.VMEM((heads * cols, nope), BF16),
                pltpu.VMEM((heads * cols, width), BF16),
                pltpu.VMEM(out_weight.shape[::-1], BF16),
                pltpu.VMEM((latent, positions), BF16),
                pltpu.VMEM((width, heads * cols), BF16),
                pltpu.VMEM((positions, rows), F32),
                pltpu.VMEM((n, cols, rows), BF16),
                pltpu.VMEM((n, 2, rows), F32),
                pltpu.VMEM((n, cols, rows), BF16),
                pltpu.VMEM((n, cols, rows), BF16),
                pltpu.VMEM((n, width // n, rows), BF16),
                pltpu.VMEM((n, width // n, rows), BF16),
                pltpu.VMEM((n, width // n, rows), BF16),
                pltpu.VMEM((drafts, heads * width), BF16),
                pltpu.VMEM((drafts, heads, width), F32),
                pltpu.VMEM((groups, drafts, model), F32),
                dma((7,)),
            ]
            + [dma((n,))] * 11
            + [dma((groups,))] * 2,
            compiler_params=pltpu.CompilerParams(
                collective_id=0, has_side_effects=True, vmem_limit_bytes=63 * 1024 * 1024
            ),
        )(
            query_nope.reshape(rows, nope),
            query_rope.reshape(rows, rope),
            latent_cache.reshape(positions, latent),
            rope_keys.reshape(rope, positions),
            lengths,
            key_quant.reshape(heads * cols, nope),
            key_scale.T,
            value_quant.reshape(heads * cols, width),
            value_scale.T,
            out_weight.T,
        )
        return result.reshape(batch, drafts, model)

    in_specs = (
        P(None, None, "heads", None),
        P(None, None, "heads", None),
        P(None, "seq", None),
        P(None, None, "seq"),
        P(),
        P("heads", "seq", None),
        P("heads", None),
        P("heads", "seq", None),
        P("heads", None),
        P("heads", "seq"),
    )
    return jax.shard_map(
        per_device, mesh=mesh, in_specs=in_specs, out_specs=P(None, None, "seq"), check_vma=False
    )
```

profile of v0, /device:TPU:0, one launch (start us, length us, event | category | flops | bytes accessed | tf_op | source)
XLA Modules:
  0.0 39.9 jit_solution(13671782492467011072)
XLA Ops:
  0.7 37.9 %shard_map.100 = bf16[4,448]{1,0:T(4,128)(2,1)} custom-call(bf16[256,128]{1,0:T(8,128)(2,1)} %bitcast.14, bf16[256,64]{1,0:T(8,128)(2,1)} %bitcast.15, bf16[512,512]{1,0:T(8,128)(2,1)} %bitcast.11, bf16[64,512]{1,0:T(8,128)(2,1)} %bitcast.16, s32[1]{0:T(128)S(6)} %copy.12.len_ref, bf16[2048,128]{1,0:T(8,128)(2,1)} %bitcast.12, f32[4,64]{1,0:T(4,128)} %bitcast.18, ...), custom_call_target="tpu_custom_call" | custom-call | tf_op jit(solution)/shard_map/pallas_call | solution.py:325
  38.6 1.3 %copy.13 = bf16[1,4,448]{2,1,0:T(4,128)(2,1)} copy(bf16[1,4,448]{2,1,0:T(4,128)(2,1)} %bitcast.17) | data formatting | bytes 7168
where the time goes:
time: 40.1 us; the launch traced here: 39.9 us
  Pallas kernels  37.9 us (95%)
  local copies, waits for them, and re-layouts  1.28 us (3%)
  between operations  0.66 us (2%)
    pallas_call x1, Pallas kernels, per_device(): pl.pallas_call(functools.partial(kernel, n, groups, heads, drafts), out_s...  37.9 us
    unnamed x1, local copies, waits for them, and re-layouts  1.28 us

commit v1 on v0

--- a/solution.py
+++ b/solution.py
@@ -295,11 +295,450 @@
         pair(j, True).wait_send()
 
 
+def chip_peer(chip, chips, k):
+    out = 0
+    bit = 1
+    while bit < chips:
+        own = lax.rem(chip // bit, 2)
+        out = out + bit * ((1 - own) if k & bit else own)
+        bit *= 2
+    return out
+
+
+def pair_kernel(
+    n,
+    groups,
+    heads,
+    drafts,
+    q_hbm,
+    qr_hbm,
+    cache_hbm,
+    rope_hbm,
+    len_ref,
+    kq_hbm,
+    ks_ref,
+    vq_hbm,
+    vs_ref,
+    w_hbm,
+    out_ref,
+    q,
+    qr,
+    cache,
+    rope,
+    kq,
+    vq,
+    w,
+    q_rows,
+    qr_rows,
+    cache_t,
+    base,
+    lat_send,
+    lat_all,
+    st_send,
+    st_all,
+    out_send,
+    out_recv,
+    part_send,
+    part_recv,
+    share_send,
+    share_recv,
+    fin_send,
+    fin_recv,
+    in_sem,
+    swap_s,
+    swap_r,
+    lat_s,
+    lat_ps,
+    lat_r,
+    st_s,
+    st_r,
+    o_s,
+    o_r,
+    p_s,
+    p_r,
+    s_s,
+    s_r,
+    f_s,
+    f_r,
+):
+    me = lax.axis_index("seq")
+    group = lax.axis_index("heads")
+    core = lax.rem(me, 2)
+    other = 1 - core
+    chip = me // 2
+    chips = n // 2
+    half = heads // 2
+    rows = half * drafts
+    cols = lat_all.shape[1]
+    wide = 2 * cols
+    latent = cache.shape[2]
+    positions = cache.shape[1]
+    width = vq.shape[2]
+    span = half * width
+    share = rows // chips
+    per = share // drafts
+    factor = (q.shape[2] + qr.shape[2]) ** (-0.5)
+    far_first = range(chips - 1, -1, -1)
+    peers = [chip_peer(chip, chips, k) for k in range(chips)]
+    partner = 2 * chip + other
+
+    barrier = pltpu.get_barrier_semaphore()
+    for k in far_first:
+        for b in range(2):
+            if k:
+                pl.semaphore_signal(barrier, inc=1, device_id=(group, 2 * peers[k] + b), device_id_type=MESH)
+    pl.semaphore_signal(barrier, inc=1, device_id=(group, partner), device_id_type=MESH)
+    for j in range(1, groups):
+        for b in range(2):
+            pl.semaphore_signal(
+                barrier, inc=1, device_id=(lax.rem(group + j, groups), 2 * chip + b), device_id_type=MESH
+            )
+
+    def local(i, src, dst):
+        copy = pltpu.make_async_copy(src, dst, in_sem.at[i])
+        copy.start()
+        return copy
+
+    q_load = local(0, q_hbm, q)
+    kq_loads = [local(1 + b, kq_hbm.at[pl.ds(b * half, half)], kq.at[pl.ds(b * half, half)]) for b in range(2)]
+    qr_load = local(3, qr_hbm.at[:, pl.ds(core * half, half)], qr)
+    rope_load = local(4, rope_hbm, rope.at[core])
+    cache_load = local(5, cache_hbm, cache.at[core])
+
+    def remote(src, dst, send, recv, peer_group, peer):
+        return pltpu.make_async_remote_copy(
+            src_ref=src,
+            dst_ref=dst,
+            send_sem=send,
+            recv_sem=recv,
+            device_id=(peer_group, peer),
+            device_id_type=MESH,
+        )
+
+    lane = lax.broadcasted_iota(jnp.int32, (1, rows), 1)
+    block = (me * cols) // QB
+
+    def scale_line(scale_ref, index):
+        scales = scale_ref[...]
+        at = lax.broadcasted_iota(jnp.int32, scales.shape, 0) == index
+        return jnp.sum(jnp.where(at, scales, 0.0), axis=0, keepdims=True)
+
+    def scale_column(line, count, first, step):
+        shape = (count, heads)
+        pick = lax.broadcasted_iota(jnp.int32, shape, 1) == lax.broadcasted_iota(jnp.int32, shape, 0) // step + first
+        return jnp.sum(jnp.where(pick, line, 0.0), axis=1, keepdims=True)
+
+    key_column = scale_column(scale_line(ks_ref, block), heads, 0, 1)
+    own_head = lax.broadcasted_iota(jnp.int32, (half, rows), 0) == lane // drafts
+    key_rows = [
+        jnp.sum(jnp.where(own_head, key_column[b * half : (b + 1) * half], 0.0), axis=0, keepdims=True)
+        for b in range(2)
+    ]
+    value_column = scale_column(scale_line(vs_ref, block), rows, other * half, drafts)
+
+    q_load.wait()
+    for b in range(2):
+        for t in range(drafts):
+            q_rows[b, pl.ds(t, half, stride=drafts), :] = q[t, b * half : (b + 1) * half, :].astype(F32)
+
+    own = lax.broadcasted_iota(jnp.int32, (half, 1, rows), 0) == lane[None] // drafts
+    for b in range(2):
+        kq_loads[b].wait()
+        every = lax.dot_general(
+            kq[b * half : (b + 1) * half].reshape(half * cols, kq.shape[2]),
+            q_rows[b].astype(BF16),
+            (((1,), (1,)), ((), ())),
+            preferred_element_type=F32,
+        ).reshape(half, cols, rows)
+        lat_send[b] = (jnp.sum(jnp.where(own, every, 0.0), axis=0) * key_rows[b]).astype(BF16)
+        if b == 0:
+            pl.semaphore_wait(barrier, n - 1 + 2 * (groups - 1))
+        for k in far_first:
+            if k:
+                remote(
+                    lat_send.at[b], lat_all.at[me], lat_s.at[b, k], lat_r.at[me], group, 2 * peers[k] + b
+                ).start()
+    lat_pair = remote(lat_send.at[other], lat_all.at[me], lat_ps, lat_r.at[me], group, partner)
+    lat_pair.start()
+    lat_all[me] = lat_send[core]
+
+    swaps = [
+        remote(src, dst, swap_s.at[i], swap_r.at[i], group, partner)
+        for i, (src, dst) in enumerate(
+            (
+                (rope_hbm, rope.at[core]),
+                (cache_hbm, cache.at[core]),
+                (vq_hbm.at[pl.ds(core * half, half)], vq.at[:, pl.ds(core * cols, cols)]),
+                (w_hbm.at[:, pl.ds(core * span, span)], w.at[core]),
+            )
+        )
+    ]
+    swap_arrive = [
+        remote(src, dst, swap_s.at[i], swap_r.at[i], group, partner)
+        for i, (src, dst) in enumerate(
+            (
+                (rope_hbm, rope.at[other]),
+                (cache_hbm, cache.at[other]),
+                (vq_hbm.at[pl.ds(core * half, half)], vq.at[:, pl.ds(other * cols, cols)]),
+                (w_hbm.at[:, pl.ds(core * span, span)], w.at[other]),
+            )
+        )
+    ]
+    for each in swaps:
+        each.start()
+    vq_load = local(6, vq_hbm.at[pl.ds(other * half, half)], vq.at[:, pl.ds(core * cols, cols)])
+    w_load = local(7, w_hbm.at[:, pl.ds(other * span, span)], w.at[core])
+
+    qr_load.wait()
+    for t in range(drafts):
+        qr_rows[pl.ds(t, half, stride=drafts), :] = qr[t].astype(F32)
+    query_rope = qr_rows[...].astype(BF16)
+
+    def prepare(j):
+        turned = lax.dot_general(
+            rope[j].T, query_rope, (((1,), (1,)), ((), ())), preferred_element_type=F32
+        )
+        position = (2 * chip + j) * positions + lax.broadcasted_iota(jnp.int32, (positions, rows), 0)
+        horizon = len_ref[0] + lax.rem(lax.broadcasted_iota(jnp.int32, (positions, rows), 1), drafts)
+        base[j] = jnp.where(position < horizon, turned * factor, neg_large)
+        cache_t[j] = cache[j].T
+
+    rope_load.wait()
+    cache_load.wait()
+    prepare(core)
+    swap_arrive[0].wait_recv()
+    swap_arrive[1].wait_recv()
+    prepare(other)
+
+    def lat_wait(k):
+        for b in range(2):
+            src = 2 * peers[k] + b
+            remote(lat_send.at[b], lat_all.at[src], lat_s.at[b, k], lat_r.at[src], group, src).wait_recv()
+
+    quarter = chips // 2
+    near = chip // quarter
+    remote(lat_send.at[other], lat_all.at[partner], lat_ps, lat_r.at[partner], group, partner).wait_recv()
+    for k in range(1, quarter):
+        lat_wait(k)
+
+    def part_scores(side):
+        begin = pl.multiple_of(side * (latent // 2), latent // 2)
+        query = lat_all[pl.ds(side * chips, chips)].reshape(latent // 2, rows)
+        return [
+            jnp.dot(cache[j, :, pl.ds(begin, latent // 2)], query, preferred_element_type=F32) * factor + base[j]
+            for j in range(2)
+        ]
+
+    for j, each in enumerate(part_scores(near)):
+        base[j] = each
+    for k in range(quarter, chips):
+        lat_wait(k)
+    scores = part_scores(1 - near)
+    block_max = jnp.maximum(
+        jnp.max(scores[0], axis=0, keepdims=True), jnp.max(scores[1], axis=0, keepdims=True)
+    )
+    probs = [jnp.exp(each - block_max) for each in scores]
+    st_send[0:1, :] = block_max
+    st_send[1:2, :] = jnp.sum(probs[0], axis=0, keepdims=True) + jnp.sum(probs[1], axis=0, keepdims=True)
+
+    def exchange(src_of, dst, send, recv, ks):
+        for k in ks:
+            remote(src_of(k), dst.at[k], send.at[k], recv.at[k], group, 2 * peers[k] + other).start()
+
+    def arrive(src_of, dst, send, recv, k):
+        remote(src_of(k), dst.at[k], send.at[k], recv.at[k], group, 2 * peers[k] + other).wait_recv()
+
+    st = (lambda k: st_send, st_all, st_s, st_r)
+    exchange(*st, far_first)
+    probs = [each.astype(BF16) for each in probs]
+    o = (lambda k: out_send.at[peers[k]], out_recv, o_s, o_r)
+    for side, ks in ((1 - near, range(chips - 1, quarter - 1, -1)), (near, range(quarter - 1, -1, -1))):
+        begin = pl.multiple_of(side * (latent // 2), latent // 2)
+        block_out = sum(
+            jnp.dot(cache_t[j, pl.ds(begin, latent // 2), :], probs[j], preferred_element_type=F32)
+            for j in range(2)
+        )
+        out_send[pl.ds(side * quarter, quarter)] = block_out.astype(BF16).reshape(quarter, wide, rows)
+        exchange(*o, ks)
+
+    vq_load.wait()
+    swap_arrive[2].wait_recv()
+
+    for k in range(chips):
+        arrive(*st, k)
+    all_max = [st_all[k, 0:1, :] for k in range(chips)]
+    top = functools.reduce(jnp.maximum, all_max)
+    weight = [jnp.exp(each - top) for each in all_max]
+    total = sum(weight[k] * st_all[k, 1:2, :] for k in range(chips))
+    merged = jnp.zeros((wide, rows), F32)
+    for k in range(chips):
+        arrive(*o, k)
+        merged = merged + out_recv[k].astype(F32) * weight[k]
+    merged = (merged / total).astype(BF16).astype(F32).T
+    tile = per * wide
+    spread = jnp.concatenate([merged] * per, axis=1)
+    keep = (
+        lax.broadcasted_iota(jnp.int32, (rows, tile), 1) // wide
+        == lax.rem(lax.broadcasted_iota(jnp.int32, (rows, tile), 0) // drafts, per)
+    )
+    spread = jnp.where(keep, spread, 0.0).astype(BF16)
+    for e in range(chips):
+        part = jnp.dot(
+            spread[e * share : (e + 1) * share],
+            vq[e * per : (e + 1) * per].reshape(tile, width),
+            preferred_element_type=F32,
+        )
+        part_send[e] = (part * value_column[e * share : (e + 1) * share]).astype(BF16)
+    p = (lambda k: part_send.at[peers[k]], part_recv, p_s, p_r)
+    exchange(*p, far_first)
+    summed = jnp.zeros((share, width), F32)
+    for k in range(chips):
+        arrive(*p, k)
+        summed = summed + part_recv[k].astype(F32)
+    for h in range(per):
+        share_send[:, h * width : (h + 1) * width] = summed[h * drafts : (h + 1) * drafts].astype(BF16)
+    s = (lambda k: share_send, share_recv, s_s, s_r)
+    exchange(*s, far_first)
+
+    w_load.wait()
+    swap_arrive[3].wait_recv()
+    model = w.shape[1]
+    final = [jnp.zeros((drafts, model), F32) for j in range(2)]
+    for k in range(chips):
+        arrive(*s, k)
+        begin = pl.multiple_of(peers[k] * (per * width), per * width)
+        for j in range(2):
+            final[j] = final[j] + lax.dot_general(
+                share_recv[k],
+                w[j, :, pl.ds(begin, per * width)],
+                (((1,), (1,)), ((), ())),
+                preferred_element_type=F32,
+            )
+    for j in range(2):
+        fin_send[j] = final[j]
+
+    def last(i, j, b):
+        peer_group = lax.rem(group + j, groups)
+        side = core if b == 0 else other
+        return remote(fin_send.at[side], fin_recv.at[i], f_s.at[i], f_r.at[i], peer_group, 2 * chip + side)
+
+    lasts = [last(i, j, b) for i, (j, b) in enumerate((j, b) for j in range(groups) for b in range(2) if j or b)]
+    for each in lasts[::-1]:
+        each.start()
+    result = fin_send[core]
+    back = [((-j) % groups, b) for j in range(groups) for b in range(2) if j or b]
+    for i in range(len(lasts)):
+        lasts[i].wait_recv()
+        result = result + fin_recv[i]
+    out_ref[...] = result.astype(BF16)
+
+    for src_of, dst, send, recv in (st, o, p, s):
+        for k in range(chips):
+            remote(src_of(k), dst.at[k], send.at[k], recv.at[k], group, 2 * peers[k] + other).wait_send()
+    for b in range(2):
+        for k in range(1, chips):
+            remote(
+                lat_send.at[b], lat_all.at[me], lat_s.at[b, k], lat_r.at[me], group, 2 * peers[k] + b
+            ).wait_send()
+    lat_pair.wait_send()
+    for each in swaps:
+        each.wait_send()
+    for each in lasts:
+        each.wait_send()
+
+
 def solution(mesh):
     n = mesh.shape["seq"]
     groups = mesh.shape["heads"]
 
-    def per_device(
+    def paired(query_nope, query_rope, latent_cache, rope_keys, lengths, key_quant, key_scale, value_quant, value_scale, out_weight):
+        drafts, heads, nope = query_nope.shape[1:]
+        rope = query_rope.shape[-1]
+        positions, latent = latent_cache.shape[1:]
+        cols = key_quant.shape[1]
+        width = value_quant.shape[2]
+        model = out_weight.shape[1]
+        chips = n // 2
+        half = heads // 2
+        rows = half * drafts
+        share = rows // chips
+        wide = 2 * cols
+        hbm = pl.BlockSpec(memory_space=pltpu.HBM)
+        vmem = pl.BlockSpec(memory_space=pltpu.VMEM)
+        smem = pl.BlockSpec(memory_space=pltpu.SMEM)
+        dma = pltpu.SemaphoreType.DMA
+        lasts = 2 * groups - 1
+        result = pl.pallas_call(
+            functools.partial(pair_kernel, n, groups, heads, drafts),
+            out_shape=jax.ShapeDtypeStruct((drafts, model), BF16),
+            in_specs=[hbm, hbm, hbm, hbm, smem, hbm, vmem, hbm, vmem, hbm],
+            out_specs=vmem,
+            scratch_shapes=[
+                pltpu.VMEM((drafts, heads, nope), BF16),
+                pltpu.VMEM((drafts, half, rope), BF16),
+                pltpu.VMEM((2, positions, latent), BF16),
+                pltpu.VMEM((2, rope, positions), BF16),
+                pltpu.VMEM((heads, cols, nope), BF16),
+                pltpu.VMEM((half, wide, width), BF16),
+                pltpu.VMEM((2, model, half * width), BF16),
+                pltpu.VMEM((2, rows, nope), F32),
+                pltpu.VMEM((rows, rope), F32),
+                pltpu.VMEM((2, latent, positions), BF16),
+                pltpu.VMEM((2, positions, rows), F32),
+                pltpu.VMEM((2, cols, rows), BF16),
+                pltpu.VMEM((n, cols, rows), BF16),
+                pltpu.VMEM((2, rows), F32),
+                pltpu.VMEM((chips, 2, rows), F32),
+                pltpu.VMEM((chips, wide, rows), BF16),
+                pltpu.VMEM((chips, wide, rows), BF16),
+                pltpu.VMEM((chips, share, width), BF16),
+                pltpu.VMEM((chips, share, width), BF16),
+                pltpu.VMEM((drafts, share // drafts * width), BF16),
+                pltpu.VMEM((chips, drafts, share // drafts * width), BF16),
+                pltpu.VMEM((2, drafts, model), F32),
+                pltpu.VMEM((lasts, drafts, model), F32),
+                dma((8,)),
+                dma((4,)),
+                dma((4,)),
+                dma((2, chips)),
+                dma,
+                dma((n,)),
+            ]
+            + [dma((chips,))] * 8
+            + [dma((lasts,))] * 2,
+            compiler_params=pltpu.CompilerParams(
+                collective_id=0, has_side_effects=True, vmem_limit_bytes=63 * 1024 * 1024
+            ),
+        )(
+            query_nope.reshape(drafts, heads, nope),
+            query_rope.reshape(drafts, heads, rope),
+            latent_cache.reshape(positions, latent),
+            rope_keys.reshape(rope, positions),
+            lengths,
+            key_quant,
+            key_scale.T,
+            value_quant,
+            value_scale.T,
+            out_weight.T,
+        )
+        return result.reshape(1, drafts, model)
+
+    def per_device(*args):
+        drafts, heads = args[0].shape[1:3]
+        chips = n // 2
+        rows = heads // 2 * drafts
+        paired_fits = (
+            n % 2 == 0
+            and chips & (chips - 1) == 0
+            and chips >= 2
+            and heads % (2 * chips) == 0
+            and rows % 128 == 0
+            and args[5].shape[1] % 16 == 0
+            and QB % (2 * args[5].shape[1]) == 0
+        )
+        return (paired if paired_fits else spread_out)(*args)
+
+    def spread_out(
         query_nope,
         query_rope,
         latent_cache,

time: 40.1 us -> 32.3 us (0.81)
  Pallas kernels: 37.9 us -> 30.2 us
    pallas_call x1, Pallas kernels: 37.9 us -> 30.2 us  [paired(): pl.pallas_call(functools.partial(pair_kernel, n, groups, heads, drafts),...]
where the time goes in v1:
time: 32.3 us; the launch traced here: 32.1 us
  Pallas kernels  30.2 us (93%)
  local copies, waits for them, and re-layouts  1.28 us (4%)
  between operations  0.66 us (2%)
    pallas_call x1, Pallas kernels, paired(): pl.pallas_call(functools.partial(pair_kernel, n, groups, heads, drafts),...  30.2 us
    unnamed x1, local copies, waits for them, and re-layouts  1.28 us

profile of v1, /device:TPU:0, one launch (start us, length us, event | category | flops | bytes accessed | tf_op | source)
XLA Modules:
  0.0 32.1 jit_solution(17583846767549311463)
XLA Ops:
  0.7 30.2 %shard_map.100 = bf16[4,448]{1,0:T(4,128)(2,1)} custom-call(bf16[4,64,128]{2,1,0:T(8,128)(2,1)} %bitcast.10, bf16[4,64,64]{2,1,0:T(8,128)(2,1)} %bitcast.11, bf16[512,512]{1,0:T(8,128)(2,1)} %bitcast.9, bf16[64,512]{1,0:T(8,128)(2,1)} %bitcast.12, s32[1]{0:T(128)S(6)} %copy.12.len_ref, bf16[64,32,128]{2,1,0:T(8,128)(2,1)} %kq_hbm.1, f32[4,64]{1,0:T(4,128)} %bitcast.14, ...), custom_call_target="tpu_custom_call" | custom-call | tf_op jit(solution)/shard_map/pallas_call | solution.py:671
  30.8 1.3 %copy.13 = bf16[1,4,448]{2,1,0:T(4,128)(2,1)} copy(bf16[1,4,448]{2,1,0:T(4,128)(2,1)} %bitcast.13) | data formatting | bytes 7168

commit v2 on v1

--- a/solution.py
+++ b/solution.py
@@ -8,6 +8,7 @@
 from jax.sharding import PartitionSpec as P
 
 QB = 128
+VMEM_LIMIT = 67043328 - 32768
 MESH = pl.DeviceIdType.MESH
 neg_large = -1e30
 F32 = jnp.float32
@@ -314,13 +315,16 @@
     qr_hbm,
     cache_hbm,
     rope_hbm,
-    len_ref,
+    len_hbm,
     kq_hbm,
-    ks_ref,
+    ks_hbm,
     vq_hbm,
-    vs_ref,
+    vs_hbm,
     w_hbm,
     out_ref,
+    len_ref,
+    ks_ref,
+    vs_ref,
     q,
     qr,
     cache,
@@ -399,11 +403,14 @@
         copy.start()
         return copy
 
+    ks_load = local(8, ks_hbm, ks_ref)
     q_load = local(0, q_hbm, q)
     kq_loads = [local(1 + b, kq_hbm.at[pl.ds(b * half, half)], kq.at[pl.ds(b * half, half)]) for b in range(2)]
     qr_load = local(3, qr_hbm.at[:, pl.ds(core * half, half)], qr)
     rope_load = local(4, rope_hbm, rope.at[core])
     cache_load = local(5, cache_hbm, cache.at[core])
+    vs_load = local(9, vs_hbm, vs_ref)
+    len_load = local(10, len_hbm, len_ref)
 
     def remote(src, dst, send, recv, peer_group, peer):
         return pltpu.make_async_remote_copy(
@@ -428,13 +435,13 @@
         pick = lax.broadcasted_iota(jnp.int32, shape, 1) == lax.broadcasted_iota(jnp.int32, shape, 0) // step + first
         return jnp.sum(jnp.where(pick, line, 0.0), axis=1, keepdims=True)
 
+    ks_load.wait()
     key_column = scale_column(scale_line(ks_ref, block), heads, 0, 1)
     own_head = lax.broadcasted_iota(jnp.int32, (half, rows), 0) == lane // drafts
     key_rows = [
         jnp.sum(jnp.where(own_head, key_column[b * half : (b + 1) * half], 0.0), axis=0, keepdims=True)
         for b in range(2)
     ]
-    value_column = scale_column(scale_line(vs_ref, block), rows, other * half, drafts)
 
     q_load.wait()
     for b in range(2):
@@ -503,6 +510,9 @@
         base[j] = jnp.where(position < horizon, turned * factor, neg_large)
         cache_t[j] = cache[j].T
 
+    vs_load.wait()
+    value_column = scale_column(scale_line(vs_ref, block), rows, other * half, drafts)
+    len_load.wait()
     rope_load.wait()
     cache_load.wait()
     prepare(core)
@@ -665,15 +675,17 @@
         wide = 2 * cols
         hbm = pl.BlockSpec(memory_space=pltpu.HBM)
         vmem = pl.BlockSpec(memory_space=pltpu.VMEM)
-        smem = pl.BlockSpec(memory_space=pltpu.SMEM)
         dma = pltpu.SemaphoreType.DMA
         lasts = 2 * groups - 1
         result = pl.pallas_call(
             functools.partial(pair_kernel, n, groups, heads, drafts),
-            out_shape=jax.ShapeDtypeStruct((drafts, model), BF16),
-            in_specs=[hbm, hbm, hbm, hbm, smem, hbm, vmem, hbm, vmem, hbm],
+            out_shape=pltpu.VMEM((drafts, model), BF16),
+            in_specs=[hbm] * 10,
             out_specs=vmem,
             scratch_shapes=[
+                pltpu.SMEM(lengths.shape, jnp.int32),
+                pltpu.VMEM(key_scale.shape[::-1], F32),
+                pltpu.VMEM(value_scale.shape[::-1], F32),
                 pltpu.VMEM((drafts, heads, nope), BF16),
                 pltpu.VMEM((drafts, half, rope), BF16),
                 pltpu.VMEM((2, positions, latent), BF16),
@@ -697,7 +709,7 @@
                 pltpu.VMEM((chips, drafts, share // drafts * width), BF16),
                 pltpu.VMEM((2, drafts, model), F32),
                 pltpu.VMEM((lasts, drafts, model), F32),
-                dma((8,)),
+                dma((11,)),
                 dma((4,)),
                 dma((4,)),
                 dma((2, chips)),
@@ -707,7 +719,7 @@
             + [dma((chips,))] * 8
             + [dma((lasts,))] * 2,
             compiler_params=pltpu.CompilerParams(
-                collective_id=0, has_side_effects=True, vmem_limit_bytes=63 * 1024 * 1024
+                collective_id=0, has_side_effects=True, vmem_limit_bytes=VMEM_LIMIT
             ),
         )(
             query_nope.reshape(drafts, heads, nope),

time: 32.3 us -> 30.4 us (0.941)
  Pallas kernels: 30.2 us -> 29 us
  local copies, waits for them, and re-layouts: 1.28 us -> 0.6 us
    pallas_call x1, Pallas kernels: 30.2 us -> 29 us  [paired(): pl.pallas_call(functools.partial(pair_kernel, n, groups, heads, drafts),...]
    unnamed x1, local copies, waits for them, and re-layouts: 1.28 us -> 0.6 us
where the time goes in v2:
time: 30.4 us; the launch traced here: 30.2 us
  Pallas kernels  29 us (95%)
  between operations  0.66 us (2%)
  local copies, waits for them, and re-layouts  0.6 us (2%)
    pallas_call x1, Pallas kernels, paired(): pl.pallas_call(functools.partial(pair_kernel, n, groups, heads, drafts),...  29 us

profile of v2, /device:TPU:0, one launch (start us, length us, event | category | flops | bytes accessed | tf_op | source)
XLA Modules:
  0.0 30.2 jit_solution(1681138510513348826)
XLA Ops:
  0.7 29.0 %shard_map.100 = bf16[4,448]{1,0:T(4,128)(2,1)S(1)} custom-call(bf16[4,64,128]{2,1,0:T(8,128)(2,1)} %bitcast.11, bf16[4,64,64]{2,1,0:T(8,128)(2,1)} %bitcast.12, bf16[512,512]{1,0:T(8,128)(2,1)} %bitcast.10, bf16[64,512]{1,0:T(8,128)(2,1)} %bitcast.13, s32[1]{0:T(128)S(6)} %copy.13.len_hbm, bf16[64,32,128]{2,1,0:T(8,128)(2,1)} %kq_hbm.1, f32[4,64]{1,0:T(4,128)} %bitcast.14, ...), custom_call_target="tpu_custom_call" | custom-call | tf_op jit(solution)/shard_map/pallas_call | solution.py:680
  29.6 0.6 %copy.12 = bf16[1,4,448]{2,1,0:T(4,128)(2,1)} copy(bf16[1,4,448]{2,1,0:T(4,128)(2,1)S(1)} %bitcast.8) | data formatting | bytes 7168

commit v3 on v2

--- a/solution.py
+++ b/solution.py
@@ -352,7 +352,6 @@
     swap_s,
     swap_r,
     lat_s,
-    lat_ps,
     lat_r,
     st_s,
     st_r,
@@ -385,6 +384,16 @@
     far_first = range(chips - 1, -1, -1)
     peers = [chip_peer(chip, chips, k) for k in range(chips)]
     partner = 2 * chip + other
+    quarter = chips // 2
+    near = chip // quarter
+
+    def local(i, src, dst):
+        copy = pltpu.make_async_copy(src, dst, in_sem.at[i])
+        copy.start()
+        return copy
+
+    q_load = local(0, q_hbm, q)
+    kq_loads = [local(1 + b, kq_hbm.at[pl.ds(b * half, half)], kq.at[pl.ds(b * half, half)]) for b in range(2)]
 
     barrier = pltpu.get_barrier_semaphore()
     for k in far_first:
@@ -398,14 +407,7 @@
                 barrier, inc=1, device_id=(lax.rem(group + j, groups), 2 * chip + b), device_id_type=MESH
             )
 
-    def local(i, src, dst):
-        copy = pltpu.make_async_copy(src, dst, in_sem.at[i])
-        copy.start()
-        return copy
-
     ks_load = local(8, ks_hbm, ks_ref)
-    q_load = local(0, q_hbm, q)
-    kq_loads = [local(1 + b, kq_hbm.at[pl.ds(b * half, half)], kq.at[pl.ds(b * half, half)]) for b in range(2)]
     qr_load = local(3, qr_hbm.at[:, pl.ds(core * half, half)], qr)
     rope_load = local(4, rope_hbm, rope.at[core])
     cache_load = local(5, cache_hbm, cache.at[core])
@@ -463,10 +465,9 @@
         for k in far_first:
             if k:
                 remote(
-                    lat_send.at[b], lat_all.at[me], lat_s.at[b, k], lat_r.at[me], group, 2 * peers[k] + b
+                    lat_send.at[b], lat_all.at[me], lat_s, lat_r.at[k // quarter], group, 2 * peers[k] + b
                 ).start()
-    lat_pair = remote(lat_send.at[other], lat_all.at[me], lat_ps, lat_r.at[me], group, partner)
-    lat_pair.start()
+    remote(lat_send.at[other], lat_all.at[me], lat_s, lat_r.at[0], group, partner).start()
     lat_all[me] = lat_send[core]
 
     swaps = [
@@ -520,16 +521,11 @@
     swap_arrive[1].wait_recv()
     prepare(other)
 
-    def lat_wait(k):
-        for b in range(2):
-            src = 2 * peers[k] + b
-            remote(lat_send.at[b], lat_all.at[src], lat_s.at[b, k], lat_r.at[src], group, src).wait_recv()
-
-    quarter = chips // 2
-    near = chip // quarter
-    remote(lat_send.at[other], lat_all.at[partner], lat_ps, lat_r.at[partner], group, partner).wait_recv()
-    for k in range(1, quarter):
-        lat_wait(k)
+    def pieces(ref, count, send, recv):
+        some = ref.at[pl.ds(0, count)]
+        return remote(some, some, send, recv, group, partner)
+
+    pieces(lat_all, 2 * quarter - 1, lat_s, lat_r.at[0]).wait_recv()
 
     def part_scores(side):
         begin = pl.multiple_of(side * (latent // 2), latent // 2)
@@ -541,8 +537,7 @@
 
     for j, each in enumerate(part_scores(near)):
         base[j] = each
-    for k in range(quarter, chips):
-        lat_wait(k)
+    pieces(lat_all, 2 * quarter, lat_s, lat_r.at[1]).wait_recv()
     scores = part_scores(1 - near)
     block_max = jnp.maximum(
         jnp.max(scores[0], axis=0, keepdims=True), jnp.max(scores[1], axis=0, keepdims=True)
@@ -553,15 +548,12 @@
 
     def exchange(src_of, dst, send, recv, ks):
         for k in ks:
-            remote(src_of(k), dst.at[k], send.at[k], recv.at[k], group, 2 * peers[k] + other).start()
-
-    def arrive(src_of, dst, send, recv, k):
-        remote(src_of(k), dst.at[k], send.at[k], recv.at[k], group, 2 * peers[k] + other).wait_recv()
-
-    st = (lambda k: st_send, st_all, st_s, st_r)
+            remote(src_of(k), dst.at[k], send, recv(k), group, 2 * peers[k] + other).start()
+
+    st = (lambda k: st_send, st_all, st_s, lambda k: st_r)
     exchange(*st, far_first)
     probs = [each.astype(BF16) for each in probs]
-    o = (lambda k: out_send.at[peers[k]], out_recv, o_s, o_r)
+    o = (lambda k: out_send.at[peers[k]], out_recv, o_s, lambda k: o_r.at[k // quarter])
     for side, ks in ((1 - near, range(chips - 1, quarter - 1, -1)), (near, range(quarter - 1, -1, -1))):
         begin = pl.multiple_of(side * (latent // 2), latent // 2)
         block_out = sum(
@@ -574,15 +566,15 @@
     vq_load.wait()
     swap_arrive[2].wait_recv()
 
-    for k in range(chips):
-        arrive(*st, k)
+    pieces(st_all, chips, st_s, st_r).wait_recv()
     all_max = [st_all[k, 0:1, :] for k in range(chips)]
     top = functools.reduce(jnp.maximum, all_max)
     weight = [jnp.exp(each - top) for each in all_max]
     total = sum(weight[k] * st_all[k, 1:2, :] for k in range(chips))
     merged = jnp.zeros((wide, rows), F32)
     for k in range(chips):
-        arrive(*o, k)
+        if k % quarter == 0:
+            pieces(out_recv, quarter, o_s, o_r.at[k // quarter]).wait_recv()
         merged = merged + out_recv[k].astype(F32) * weight[k]
     merged = (merged / total).astype(BF16).astype(F32).T
     tile = per * wide
@@ -599,15 +591,15 @@
             preferred_element_type=F32,
         )
         part_send[e] = (part * value_column[e * share : (e + 1) * share]).astype(BF16)
-    p = (lambda k: part_send.at[peers[k]], part_recv, p_s, p_r)
+    p = (lambda k: part_send.at[peers[k]], part_recv, p_s, lambda k: p_r)
     exchange(*p, far_first)
     summed = jnp.zeros((share, width), F32)
+    pieces(part_recv, chips, p_s, p_r).wait_recv()
     for k in range(chips):
-        arrive(*p, k)
         summed = summed + part_recv[k].astype(F32)
     for h in range(per):
         share_send[:, h * width : (h + 1) * width] = summed[h * drafts : (h + 1) * drafts].astype(BF16)
-    s = (lambda k: share_send, share_recv, s_s, s_r)
+    s = (lambda k: share_send, share_recv, s_s, lambda k: s_r.at[k])
     exchange(*s, far_first)
 
     w_load.wait()
@@ -615,7 +607,7 @@
     model = w.shape[1]
     final = [jnp.zeros((drafts, model), F32) for j in range(2)]
     for k in range(chips):
-        arrive(*s, k)
+        pieces(share_recv, 1, s_s, s_r.at[k]).wait_recv()
         begin = pl.multiple_of(peers[k] * (per * width), per * width)
         for j in range(2):
             final[j] = final[j] + lax.dot_general(
@@ -630,30 +622,27 @@
     def last(i, j, b):
         peer_group = lax.rem(group + j, groups)
         side = core if b == 0 else other
-        return remote(fin_send.at[side], fin_recv.at[i], f_s.at[i], f_r.at[i], peer_group, 2 * chip + side)
+        return remote(fin_send.at[side], fin_recv.at[i], f_s, f_r, peer_group, 2 * chip + side)
 
     lasts = [last(i, j, b) for i, (j, b) in enumerate((j, b) for j in range(groups) for b in range(2) if j or b)]
     for each in lasts[::-1]:
         each.start()
     result = fin_send[core]
-    back = [((-j) % groups, b) for j in range(groups) for b in range(2) if j or b]
+    pieces(fin_recv, len(lasts), f_s, f_r).wait_recv()
     for i in range(len(lasts)):
-        lasts[i].wait_recv()
         result = result + fin_recv[i]
     out_ref[...] = result.astype(BF16)
 
-    for src_of, dst, send, recv in (st, o, p, s):
-        for k in range(chips):
-            remote(src_of(k), dst.at[k], send.at[k], recv.at[k], group, 2 * peers[k] + other).wait_send()
-    for b in range(2):
-        for k in range(1, chips):
-            remote(
-                lat_send.at[b], lat_all.at[me], lat_s.at[b, k], lat_r.at[me], group, 2 * peers[k] + b
-            ).wait_send()
-    lat_pair.wait_send()
+    pieces(lat_all, n - 1, lat_s, lat_r.at[0]).wait_send()
+    for ref, send, recv in (
+        (st_all, st_s, st_r),
+        (out_send, o_s, o_r.at[0]),
+        (part_send, p_s, p_r),
+        (share_recv, s_s, s_r.at[0]),
+        (fin_recv, f_s, f_r),
+    ):
+        pieces(ref, ref.shape[0], send, recv).wait_send()
     for each in swaps:
-        each.wait_send()
-    for each in lasts:
         each.wait_send()
 
 
@@ -712,12 +701,19 @@
                 dma((11,)),
                 dma((4,)),
                 dma((4,)),
-                dma((2, chips)),
                 dma,
-                dma((n,)),
-            ]
-            + [dma((chips,))] * 8
-            + [dma((lasts,))] * 2,
+                dma((2,)),
+                dma,
+                dma,
+                dma,
+                dma((2,)),
+                dma,
+                dma,
+                dma,
+                dma((chips,)),
+                dma,
+                dma,
+            ],
             compiler_params=pltpu.CompilerParams(
                 collective_id=0, has_side_effects=True, vmem_limit_bytes=VMEM_LIMIT
             ),

time: 30.4 us -> 29.5 us (0.970)
  Pallas kernels: 29 us -> 28.1 us
    pallas_call x1, Pallas kernels: 29 us -> 28.1 us  [paired(): pl.pallas_call(functools.partial(pair_kernel, n, groups, heads, drafts),...]
where the time goes in v3:
time: 29.5 us; the launch traced here: 29.4 us
  Pallas kernels  28.1 us (95%)
  between operations  0.66 us (2%)
  local copies, waits for them, and re-layouts  0.6 us (2%)
    pallas_call x1, Pallas kernels, paired(): pl.pallas_call(functools.partial(pair_kernel, n, groups, heads, drafts),...  28.1 us
    unnamed x1, local copies, waits for them, and re-layouts  0.6 us

profile of v3, /device:TPU:0, one launch (start us, length us, event | category | flops | bytes accessed | tf_op | source)
XLA Modules:
  0.0 29.4 jit_solution(3693916780658036716)
XLA Ops:
  0.7 28.1 %shard_map.100 = bf16[4,448]{1,0:T(4,128)(2,1)S(1)} custom-call(bf16[4,64,128]{2,1,0:T(8,128)(2,1)} %bitcast.11, bf16[4,64,64]{2,1,0:T(8,128)(2,1)} %bitcast.12, bf16[512,512]{1,0:T(8,128)(2,1)} %bitcast.10, bf16[64,512]{1,0:T(8,128)(2,1)} %bitcast.13, s32[1]{0:T(128)S(6)} %copy.13.len_hbm, bf16[64,32,128]{2,1,0:T(8,128)(2,1)} %kq_hbm.1, f32[4,64]{1,0:T(4,128)} %bitcast.14, ...), custom_call_target="tpu_custom_call" | custom-call | tf_op jit(solution)/shard_map/pallas_call | solution.py:669
  28.8 0.6 %copy.12 = bf16[1,4,448]{2,1,0:T(4,128)(2,1)} copy(bf16[1,4,448]{2,1,0:T(4,128)(2,1)S(1)} %bitcast.8) | data formatting | bytes 7168

commit v4 on v3

--- a/solution.py
+++ b/solution.py
@@ -344,6 +344,7 @@
     out_recv,
     part_send,
     part_recv,
+    weights,
     share_send,
     share_recv,
     fin_send,
@@ -361,6 +362,8 @@
     p_r,
     s_s,
     s_r,
+    v_s,
+    v_r,
     f_s,
     f_r,
 ):
@@ -378,14 +381,15 @@
     positions = cache.shape[1]
     width = vq.shape[2]
     span = half * width
-    share = rows // chips
-    per = share // drafts
     factor = (q.shape[2] + qr.shape[2]) ** (-0.5)
     far_first = range(chips - 1, -1, -1)
     peers = [chip_peer(chip, chips, k) for k in range(chips)]
     partner = 2 * chip + other
     quarter = chips // 2
     near = chip // quarter
+    place = lax.rem(chip, quarter)
+    per = half // quarter
+    share = per * drafts
 
     def local(i, src, dst):
         copy = pltpu.make_async_copy(src, dst, in_sem.at[i])
@@ -476,7 +480,6 @@
             (
                 (rope_hbm, rope.at[core]),
                 (cache_hbm, cache.at[core]),
-                (vq_hbm.at[pl.ds(core * half, half)], vq.at[:, pl.ds(core * cols, cols)]),
                 (w_hbm.at[:, pl.ds(core * span, span)], w.at[core]),
             )
         )
@@ -487,14 +490,12 @@
             (
                 (rope_hbm, rope.at[other]),
                 (cache_hbm, cache.at[other]),
-                (vq_hbm.at[pl.ds(core * half, half)], vq.at[:, pl.ds(other * cols, cols)]),
                 (w_hbm.at[:, pl.ds(core * span, span)], w.at[other]),
             )
         )
     ]
     for each in swaps:
         each.start()
-    vq_load = local(6, vq_hbm.at[pl.ds(other * half, half)], vq.at[:, pl.ds(core * cols, cols)])
     w_load = local(7, w_hbm.at[:, pl.ds(other * span, span)], w.at[core])
 
     qr_load.wait()
@@ -512,8 +513,32 @@
         cache_t[j] = cache[j].T
 
     vs_load.wait()
-    value_column = scale_column(scale_line(vs_ref, block), rows, other * half, drafts)
+    blocks = latent // 2 // QB
+    value_scale = jnp.concatenate(
+        [
+            jnp.broadcast_to(
+                scale_column(
+                    scale_line(vs_ref, near * blocks + i), share, other * half + place * per, drafts
+                ),
+                (share, QB),
+            )
+            for i in range(blocks)
+        ],
+        axis=1,
+    )
     len_load.wait()
+    vq_slot = vq.at[:, pl.ds(place * wide + core * cols, cols)]
+
+    def vq_part(side, at):
+        return vq_hbm.at[pl.ds(side * half + at * per, per)]
+
+    vq_load = local(6, vq_part(other, place), vq_slot)
+    for k in range(quarter - 1, -1, -1):
+        for b in range(2) if k else (other,):
+            remote(
+                vq_part(1 - b, lax.rem(peers[k], quarter)), vq_slot, v_s, v_r, group, 2 * peers[k] + b
+            ).start()
+
     rope_load.wait()
     cache_load.wait()
     prepare(core)
@@ -560,55 +585,48 @@
             jnp.dot(cache_t[j, pl.ds(begin, latent // 2), :], probs[j], preferred_element_type=F32)
             for j in range(2)
         )
-        out_send[pl.ds(side * quarter, quarter)] = block_out.astype(BF16).reshape(quarter, wide, rows)
+        out_send[pl.ds(side * quarter, quarter)] = block_out.T.astype(BF16).reshape(quarter, share, latent // 2)
         exchange(*o, ks)
 
     vq_load.wait()
-    swap_arrive[2].wait_recv()
+    vq_rest = vq.at[:, pl.ds(0, (2 * quarter - 1) * cols)]
+    vq_swap = remote(vq_rest, vq_rest, v_s, v_r, group, partner)
+    vq_swap.wait_recv()
 
     pieces(st_all, chips, st_s, st_r).wait_recv()
     all_max = [st_all[k, 0:1, :] for k in range(chips)]
     top = functools.reduce(jnp.maximum, all_max)
     weight = [jnp.exp(each - top) for each in all_max]
     total = sum(weight[k] * st_all[k, 1:2, :] for k in range(chips))
-    merged = jnp.zeros((wide, rows), F32)
+    weights[...] = jnp.concatenate([each / total for each in weight], axis=0).T
+    weight = weights[pl.ds(place * share, share), :]
+    merged = jnp.zeros((share, latent // 2), F32)
     for k in range(chips):
         if k % quarter == 0:
             pieces(out_recv, quarter, o_s, o_r.at[k // quarter]).wait_recv()
-        merged = merged + out_recv[k].astype(F32) * weight[k]
-    merged = (merged / total).astype(BF16).astype(F32).T
-    tile = per * wide
-    spread = jnp.concatenate([merged] * per, axis=1)
-    keep = (
-        lax.broadcasted_iota(jnp.int32, (rows, tile), 1) // wide
-        == lax.rem(lax.broadcasted_iota(jnp.int32, (rows, tile), 0) // drafts, per)
-    )
-    spread = jnp.where(keep, spread, 0.0).astype(BF16)
-    for e in range(chips):
-        part = jnp.dot(
-            spread[e * share : (e + 1) * share],
-            vq[e * per : (e + 1) * per].reshape(tile, width),
-            preferred_element_type=F32,
-        )
-        part_send[e] = (part * value_column[e * share : (e + 1) * share]).astype(BF16)
-    p = (lambda k: part_send.at[peers[k]], part_recv, p_s, lambda k: p_r)
-    exchange(*p, far_first)
-    summed = jnp.zeros((share, width), F32)
-    pieces(part_recv, chips, p_s, p_r).wait_recv()
-    for k in range(chips):
-        summed = summed + part_recv[k].astype(F32)
+        merged = merged + out_recv[k].astype(F32) * weight[:, k : k + 1]
+    merged = (merged * value_scale).astype(BF16)
+    row_head = lax.broadcasted_iota(jnp.int32, (share, width), 0) // drafts
+    part = jnp.zeros((share, width), F32)
+    for h in range(per):
+        part = jnp.where(row_head == h, jnp.dot(merged, vq[h], preferred_element_type=F32), part)
+    part_send[...] = part.astype(BF16)
+    for i, k in ((1, quarter), (0, 0)):
+        remote(part_send, part_recv.at[i], p_s, p_r, group, 2 * peers[k] + other).start()
+    pieces(part_recv, 2, p_s, p_r).wait_recv()
+    summed = part_recv[0].astype(F32) + part_recv[1].astype(F32)
     for h in range(per):
         share_send[:, h * width : (h + 1) * width] = summed[h * drafts : (h + 1) * drafts].astype(BF16)
     s = (lambda k: share_send, share_recv, s_s, lambda k: s_r.at[k])
-    exchange(*s, far_first)
+    exchange(*s, range(quarter - 1, -1, -1))
 
     w_load.wait()
-    swap_arrive[3].wait_recv()
+    swap_arrive[2].wait_recv()
     model = w.shape[1]
     final = [jnp.zeros((drafts, model), F32) for j in range(2)]
-    for k in range(chips):
+    for k in range(quarter):
         pieces(share_recv, 1, s_s, s_r.at[k]).wait_recv()
-        begin = pl.multiple_of(peers[k] * (per * width), per * width)
+        begin = pl.multiple_of(lax.rem(peers[k], quarter) * (per * width), per * width)
         for j in range(2):
             final[j] = final[j] + lax.dot_general(
                 share_recv[k],
@@ -637,11 +655,12 @@
     for ref, send, recv in (
         (st_all, st_s, st_r),
         (out_send, o_s, o_r.at[0]),
-        (part_send, p_s, p_r),
+        (part_recv, p_s, p_r),
         (share_recv, s_s, s_r.at[0]),
         (fin_recv, f_s, f_r),
     ):
         pieces(ref, ref.shape[0], send, recv).wait_send()
+    vq_swap.wait_send()
     for each in swaps:
         each.wait_send()
 
@@ -660,8 +679,9 @@
         chips = n // 2
         half = heads // 2
         rows = half * drafts
-        share = rows // chips
-        wide = 2 * cols
+        quarter = chips // 2
+        per = half // quarter
+        share = per * drafts
         hbm = pl.BlockSpec(memory_space=pltpu.HBM)
         vmem = pl.BlockSpec(memory_space=pltpu.VMEM)
         dma = pltpu.SemaphoreType.DMA
@@ -680,7 +700,7 @@
                 pltpu.VMEM((2, positions, latent), BF16),
                 pltpu.VMEM((2, rope, positions), BF16),
                 pltpu.VMEM((heads, cols, nope), BF16),
-                pltpu.VMEM((half, wide, width), BF16),
+                pltpu.VMEM((per, latent // 2, width), BF16),
                 pltpu.VMEM((2, model, half * width), BF16),
                 pltpu.VMEM((2, rows, nope), F32),
                 pltpu.VMEM((rows, rope), F32),
@@ -690,17 +710,18 @@
                 pltpu.VMEM((n, cols, rows), BF16),
                 pltpu.VMEM((2, rows), F32),
                 pltpu.VMEM((chips, 2, rows), F32),
-                pltpu.VMEM((chips, wide, rows), BF16),
-                pltpu.VMEM((chips, wide, rows), BF16),
-                pltpu.VMEM((chips, share, width), BF16),
-                pltpu.VMEM((chips, share, width), BF16),
-                pltpu.VMEM((drafts, share // drafts * width), BF16),
-                pltpu.VMEM((chips, drafts, share // drafts * width), BF16),
+                pltpu.VMEM((chips, share, latent // 2), BF16),
+                pltpu.VMEM((chips, share, latent // 2), BF16),
+                pltpu.VMEM((share, width), BF16),
+                pltpu.VMEM((2, share, width), BF16),
+                pltpu.VMEM((rows, chips), F32),
+                pltpu.VMEM((drafts, per * width), BF16),
+                pltpu.VMEM((quarter, drafts, per * width), BF16),
                 pltpu.VMEM((2, drafts, model), F32),
                 pltpu.VMEM((lasts, drafts, model), F32),
                 dma((11,)),
-                dma((4,)),
-                dma((4,)),
+                dma((3,)),
+                dma((3,)),
                 dma,
                 dma((2,)),
                 dma,
@@ -710,7 +731,9 @@
                 dma,
                 dma,
                 dma,
-                dma((chips,)),
+                dma((quarter,)),
+                dma,
+                dma,
                 dma,
                 dma,
             ],
@@ -739,10 +762,12 @@
             n % 2 == 0
             and chips & (chips - 1) == 0
             and chips >= 2
-            and heads % (2 * chips) == 0
+            and heads % chips == 0
+            and heads // chips * drafts % 16 == 0
+            and args[2].shape[2] % (2 * QB) == 0
             and rows % 128 == 0
             and args[5].shape[1] % 16 == 0
-            and QB % (2 * args[5].shape[1]) == 0
+            and QB % args[5].shape[1] == 0
         )
         return (paired if paired_fits else spread_out)(*args)
 

time: 29.5 us -> 29.6 us (level)
  no operation moved by 1% of the time
where the time goes in v4:
time: 29.6 us; the launch traced here: 29.5 us
  Pallas kernels  28.2 us (95%)
  between operations  0.66 us (2%)
  local copies, waits for them, and re-layouts  0.6 us (2%)
    pallas_call x1, Pallas kernels, paired(): pl.pallas_call(functools.partial(pair_kernel, n, groups, heads, drafts),...  28.2 us
    unnamed x1, local copies, waits for them, and re-layouts  0.6 us

profile of v4, /device:TPU:0, one launch (start us, length us, event | category | flops | bytes accessed | tf_op | source)
XLA Modules:
  0.0 29.5 jit_solution(12209812807307096963)
XLA Ops:
  0.7 28.2 %shard_map.100 = bf16[4,448]{1,0:T(4,128)(2,1)S(1)} custom-call(bf16[4,64,128]{2,1,0:T(8,128)(2,1)} %bitcast.11, bf16[4,64,64]{2,1,0:T(8,128)(2,1)} %bitcast.12, bf16[512,512]{1,0:T(8,128)(2,1)} %bitcast.10, bf16[64,512]{1,0:T(8,128)(2,1)} %bitcast.13, s32[1]{0:T(128)S(6)} %copy.13.len_hbm, bf16[64,32,128]{2,1,0:T(8,128)(2,1)} %kq_hbm.1, f32[4,64]{1,0:T(4,128)} %bitcast.14, ...), custom_call_target="tpu_custom_call" | custom-call | tf_op jit(solution)/shard_map/pallas_call | solution.py:689
  28.9 0.6 %copy.12 = bf16[1,4,448]{2,1,0:T(4,128)(2,1)} copy(bf16[1,4,448]{2,1,0:T(4,128)(2,1)S(1)} %bitcast.8) | data formatting | bytes 7168

commit v5 on v3

--- a/solution.py
+++ b/solution.py
@@ -393,7 +393,7 @@
         return copy
 
     q_load = local(0, q_hbm, q)
-    kq_loads = [local(1 + b, kq_hbm.at[pl.ds(b * half, half)], kq.at[pl.ds(b * half, half)]) for b in range(2)]
+    kq_loads = [local(1 + b, kq_hbm.at[pl.ds(b * half, half)], kq.at[pl.ds(b * half, half)]) for b in (1, 0)][::-1]
 
     barrier = pltpu.get_barrier_semaphore()
     for k in far_first:
@@ -451,7 +451,7 @@
             q_rows[b, pl.ds(t, half, stride=drafts), :] = q[t, b * half : (b + 1) * half, :].astype(F32)
 
     own = lax.broadcasted_iota(jnp.int32, (half, 1, rows), 0) == lane[None] // drafts
-    for b in range(2):
+    for b in (1, 0):
         kq_loads[b].wait()
         every = lax.dot_general(
             kq[b * half : (b + 1) * half].reshape(half * cols, kq.shape[2]),
@@ -460,7 +460,7 @@
             preferred_element_type=F32,
         ).reshape(half, cols, rows)
         lat_send[b] = (jnp.sum(jnp.where(own, every, 0.0), axis=0) * key_rows[b]).astype(BF16)
-        if b == 0:
+        if b == 1:
             pl.semaphore_wait(barrier, n - 1 + 2 * (groups - 1))
         for k in far_first:
             if k:

time: 29.5 us -> 28.7 us (0.973)
  Pallas kernels: 28.1 us -> 27.3 us
    pallas_call x1, Pallas kernels: 28.1 us -> 27.3 us  [paired(): pl.pallas_call(functools.partial(pair_kernel, n, groups, heads, drafts),...]
where the time goes in v5:
time: 28.7 us; the launch traced here: 28.5 us
  Pallas kernels  27.3 us (95%)
  between operations  0.66 us (2%)
  local copies, waits for them, and re-layouts  0.6 us (2%)
    pallas_call x1, Pallas kernels, paired(): pl.pallas_call(functools.partial(pair_kernel, n, groups, heads, drafts),...  27.3 us
    unnamed x1, local copies, waits for them, and re-layouts  0.6 us

profile of v5, /device:TPU:0, one launch (start us, length us, event | category | flops | bytes accessed | tf_op | source)
XLA Modules:
  0.0 28.5 jit_solution(2136359097470584298)
XLA Ops:
  0.7 27.3 %shard_map.100 = bf16[4,448]{1,0:T(4,128)(2,1)S(1)} custom-call(bf16[4,64,128]{2,1,0:T(8,128)(2,1)} %bitcast.11, bf16[4,64,64]{2,1,0:T(8,128)(2,1)} %bitcast.12, bf16[512,512]{1,0:T(8,128)(2,1)} %bitcast.10, bf16[64,512]{1,0:T(8,128)(2,1)} %bitcast.13, s32[1]{0:T(128)S(6)} %copy.13.len_hbm, bf16[64,32,128]{2,1,0:T(8,128)(2,1)} %kq_hbm.1, f32[4,64]{1,0:T(4,128)} %bitcast.14, ...), custom_call_target="tpu_custom_call" | custom-call | tf_op jit(solution)/shard_map/pallas_call | solution.py:669
  27.9 0.6 %copy.12 = bf16[1,4,448]{2,1,0:T(4,128)(2,1)} copy(bf16[1,4,448]{2,1,0:T(4,128)(2,1)S(1)} %bitcast.8) | data formatting | bytes 7168

commit v6 on v5

--- a/solution.py
+++ b/solution.py
@@ -332,6 +332,7 @@
     kq,
     vq,
     w,
+    w_t,
     q_rows,
     qr_rows,
     cache_t,
@@ -563,6 +564,13 @@
         out_send[pl.ds(side * quarter, quarter)] = block_out.astype(BF16).reshape(quarter, wide, rows)
         exchange(*o, ks)
 
+    def turn(j):
+        step = per * width
+        for k in range(chips):
+            w_t[j, k * step : (k + 1) * step, :] = w[j, :, k * step : (k + 1) * step].T
+
+    w_load.wait()
+    turn(core)
     vq_load.wait()
     swap_arrive[2].wait_recv()
 
@@ -593,6 +601,8 @@
         part_send[e] = (part * value_column[e * share : (e + 1) * share]).astype(BF16)
     p = (lambda k: part_send.at[peers[k]], part_recv, p_s, lambda k: p_r)
     exchange(*p, far_first)
+    swap_arrive[3].wait_recv()
+    turn(other)
     summed = jnp.zeros((share, width), F32)
     pieces(part_recv, chips, p_s, p_r).wait_recv()
     for k in range(chips):
@@ -602,19 +612,14 @@
     s = (lambda k: share_send, share_recv, s_s, lambda k: s_r.at[k])
     exchange(*s, far_first)
 
-    w_load.wait()
-    swap_arrive[3].wait_recv()
     model = w.shape[1]
     final = [jnp.zeros((drafts, model), F32) for j in range(2)]
     for k in range(chips):
         pieces(share_recv, 1, s_s, s_r.at[k]).wait_recv()
         begin = pl.multiple_of(peers[k] * (per * width), per * width)
         for j in range(2):
-            final[j] = final[j] + lax.dot_general(
-                share_recv[k],
-                w[j, :, pl.ds(begin, per * width)],
-                (((1,), (1,)), ((), ())),
-                preferred_element_type=F32,
+            final[j] = final[j] + jnp.dot(
+                share_recv[k], w_t[j, pl.ds(begin, per * width), :], preferred_element_type=F32
             )
     for j in range(2):
         fin_send[j] = final[j]
@@ -682,6 +687,7 @@
                 pltpu.VMEM((heads, cols, nope), BF16),
                 pltpu.VMEM((half, wide, width), BF16),
                 pltpu.VMEM((2, model, half * width), BF16),
+                pltpu.VMEM((2, half * width, model), BF16),
                 pltpu.VMEM((2, rows, nope), F32),
                 pltpu.VMEM((rows, rope), F32),
                 pltpu.VMEM((2, latent, positions), BF16),

time: 28.7 us -> 27.8 us (0.969)
  Pallas kernels: 27.3 us -> 26.4 us
    pallas_call x1, Pallas kernels: 27.3 us -> 26.4 us  [paired(): pl.pallas_call(functools.partial(pair_kernel, n, groups, heads, drafts),...]
where the time goes in v6:
time: 27.8 us; the launch traced here: 27.7 us
  Pallas kernels  26.4 us (95%)
  between operations  0.66 us (2%)
  local copies, waits for them, and re-layouts  0.6 us (2%)
    pallas_call x1, Pallas kernels, paired(): pl.pallas_call(functools.partial(pair_kernel, n, groups, heads, drafts),...  26.4 us
    unnamed x1, local copies, waits for them, and re-layouts  0.6 us

profile of v6, /device:TPU:0, one launch (start us, length us, event | category | flops | bytes accessed | tf_op | source)
XLA Modules:
  0.0 27.7 jit_solution(7451653501661515218)
XLA Ops:
  0.7 26.4 %shard_map.100 = bf16[4,448]{1,0:T(4,128)(2,1)S(1)} custom-call(bf16[4,64,128]{2,1,0:T(8,128)(2,1)} %bitcast.11, bf16[4,64,64]{2,1,0:T(8,128)(2,1)} %bitcast.12, bf16[512,512]{1,0:T(8,128)(2,1)} %bitcast.10, bf16[64,512]{1,0:T(8,128)(2,1)} %bitcast.13, s32[1]{0:T(128)S(6)} %copy.13.len_hbm, bf16[64,32,128]{2,1,0:T(8,128)(2,1)} %kq_hbm.1, f32[4,64]{1,0:T(4,128)} %bitcast.14, ...), custom_call_target="tpu_custom_call" | custom-call | tf_op jit(solution)/shard_map/pallas_call | solution.py:674
  27.1 0.6 %copy.12 = bf16[1,4,448]{2,1,0:T(4,128)(2,1)} copy(bf16[1,4,448]{2,1,0:T(4,128)(2,1)S(1)} %bitcast.8) | data formatting | bytes 7168

commit v7 on v6

--- a/solution.py
+++ b/solution.py
@@ -315,14 +315,12 @@
     qr_hbm,
     cache_hbm,
     rope_hbm,
-    len_hbm,
     kq_hbm,
     ks_hbm,
     vq_hbm,
     vs_hbm,
     w_hbm,
     out_ref,
-    len_ref,
     ks_ref,
     vs_ref,
     q,
@@ -413,7 +411,6 @@
     rope_load = local(4, rope_hbm, rope.at[core])
     cache_load = local(5, cache_hbm, cache.at[core])
     vs_load = local(9, vs_hbm, vs_ref)
-    len_load = local(10, len_hbm, len_ref)
 
     def remote(src, dst, send, recv, peer_group, peer):
         return pltpu.make_async_remote_copy(
@@ -508,13 +505,12 @@
             rope[j].T, query_rope, (((1,), (1,)), ((), ())), preferred_element_type=F32
         )
         position = (2 * chip + j) * positions + lax.broadcasted_iota(jnp.int32, (positions, rows), 0)
-        horizon = len_ref[0] + lax.rem(lax.broadcasted_iota(jnp.int32, (positions, rows), 1), drafts)
+        horizon = n * positions - drafts + 1 + lax.rem(lax.broadcasted_iota(jnp.int32, (positions, rows), 1), drafts)
         base[j] = jnp.where(position < horizon, turned * factor, neg_large)
         cache_t[j] = cache[j].T
 
     vs_load.wait()
     value_column = scale_column(scale_line(vs_ref, block), rows, other * half, drafts)
-    len_load.wait()
     rope_load.wait()
     cache_load.wait()
     prepare(core)
@@ -674,10 +670,9 @@
         result = pl.pallas_call(
             functools.partial(pair_kernel, n, groups, heads, drafts),
             out_shape=pltpu.VMEM((drafts, model), BF16),
-            in_specs=[hbm] * 10,
+            in_specs=[hbm] * 9,
             out_specs=vmem,
             scratch_shapes=[
-                pltpu.SMEM(lengths.shape, jnp.int32),
                 pltpu.VMEM(key_scale.shape[::-1], F32),
                 pltpu.VMEM(value_scale.shape[::-1], F32),
                 pltpu.VMEM((drafts, heads, nope), BF16),
@@ -704,7 +699,7 @@
                 pltpu.VMEM((chips, drafts, share // drafts * width), BF16),
                 pltpu.VMEM((2, drafts, model), F32),
                 pltpu.VMEM((lasts, drafts, model), F32),
-                dma((11,)),
+                dma((10,)),
                 dma((4,)),
                 dma((4,)),
                 dma,
@@ -728,7 +723,6 @@
             query_rope.reshape(drafts, heads, rope),
             latent_cache.reshape(positions, latent),
             rope_keys.reshape(rope, positions),
-            lengths,
             key_quant,
             key_scale.T,
             value_quant,
@@ -742,7 +736,8 @@
         chips = n // 2
         rows = heads // 2 * drafts
         paired_fits = (
-            n % 2 == 0
+            args[0].shape[0] == 1
+            and n % 2 == 0
             and chips & (chips - 1) == 0
             and chips >= 2
             and heads % (2 * chips) == 0

time: 27.8 us -> 27.4 us (0.986)
  between operations: 0.66 us -> 0.01 us
  Pallas kernels: 26.4 us -> 26.7 us
where the time goes in v7:
time: 27.4 us; the launch traced here: 27.3 us
  Pallas kernels  26.7 us (97%)
  local copies, waits for them, and re-layouts  0.6 us (2%)
    pallas_call x1, Pallas kernels, paired(): pl.pallas_call(functools.partial(pair_kernel, n, groups, heads, drafts),...  26.7 us
    unnamed x1, local copies, waits for them, and re-layouts  0.6 us

profile of v7, /device:TPU:0, one launch (start us, length us, event | category | flops | bytes accessed | tf_op | source)
XLA Modules:
  0.0 27.3 jit_solution(4123570035790340391)
XLA Ops:
  0.0 26.7 %shard_map.91 = bf16[4,448]{1,0:T(4,128)(2,1)S(1)} custom-call(bf16[4,64,128]{2,1,0:T(8,128)(2,1)} %bitcast.11, bf16[4,64,64]{2,1,0:T(8,128)(2,1)} %bitcast.12, bf16[512,512]{1,0:T(8,128)(2,1)} %bitcast.10, bf16[64,512]{1,0:T(8,128)(2,1)} %bitcast.13, bf16[64,32,128]{2,1,0:T(8,128)(2,1)} %kq_hbm.1, f32[4,64]{1,0:T(4,128)} %bitcast.14, ...), custom_call_target="tpu_custom_call" | custom-call | tf_op jit(solution)/shard_map/pallas_call | solution.py:670
  26.7 0.6 %copy.11 = bf16[1,4,448]{2,1,0:T(4,128)(2,1)} copy(bf16[1,4,448]{2,1,0:T(4,128)(2,1)S(1)} %bitcast.8) | data formatting | bytes 7168

commit v8 on v7

--- a/solution.py
+++ b/solution.py
@@ -551,13 +551,16 @@
     exchange(*st, far_first)
     probs = [each.astype(BF16) for each in probs]
     o = (lambda k: out_send.at[peers[k]], out_recv, o_s, lambda k: o_r.at[k // quarter])
-    for side, ks in ((1 - near, range(chips - 1, quarter - 1, -1)), (near, range(quarter - 1, -1, -1))):
-        begin = pl.multiple_of(side * (latent // 2), latent // 2)
+    middle = quarter + quarter // 2
+    for ks in (range(middle - 1, quarter - 1, -1), range(chips - 1, middle - 1, -1), range(quarter - 1, -1, -1)):
+        count = len(ks)
+        first = count * (peers[ks[0]] // count)
+        begin = pl.multiple_of(first * wide, count * wide)
         block_out = sum(
-            jnp.dot(cache_t[j, pl.ds(begin, latent // 2), :], probs[j], preferred_element_type=F32)
+            jnp.dot(cache_t[j, pl.ds(begin, count * wide), :], probs[j], preferred_element_type=F32)
             for j in range(2)
         )
-        out_send[pl.ds(side * quarter, quarter)] = block_out.astype(BF16).reshape(quarter, wide, rows)
+        out_send[pl.ds(first, count)] = block_out.astype(BF16).reshape(count, wide, rows)
         exchange(*o, ks)
 
     def turn(j):
@@ -739,7 +742,7 @@
             args[0].shape[0] == 1
             and n % 2 == 0
             and chips & (chips - 1) == 0
-            and chips >= 2
+            and chips >= 4
             and heads % (2 * chips) == 0
             and rows % 128 == 0
             and args[5].shape[1] % 16 == 0

time: 27.4 us -> 27.1 us (0.989)
  Pallas kernels: 26.7 us -> 26.3 us
    pallas_call x1, Pallas kernels: 26.7 us -> 26.3 us  [paired(): pl.pallas_call(functools.partial(pair_kernel, n, groups, heads, drafts),...]
where the time goes in v8:
time: 27.1 us; the launch traced here: 26.9 us
  Pallas kernels  26.3 us (97%)
  local copies, waits for them, and re-layouts  0.6 us (2%)
    pallas_call x1, Pallas kernels, paired(): pl.pallas_call(functools.partial(pair_kernel, n, groups, heads, drafts),...  26.3 us
    unnamed x1, local copies, waits for them, and re-layouts  0.6 us

profile of v8, /device:TPU:0, one launch (start us, length us, event | category | flops | bytes accessed | tf_op | source)
XLA Modules:
  0.0 26.9 jit_solution(17333431104412264230)
XLA Ops:
  0.0 26.3 %shard_map.91 = bf16[4,448]{1,0:T(4,128)(2,1)S(1)} custom-call(bf16[4,64,128]{2,1,0:T(8,128)(2,1)} %bitcast.11, bf16[4,64,64]{2,1,0:T(8,128)(2,1)} %bitcast.12, bf16[512,512]{1,0:T(8,128)(2,1)} %bitcast.10, bf16[64,512]{1,0:T(8,128)(2,1)} %bitcast.13, bf16[64,32,128]{2,1,0:T(8,128)(2,1)} %kq_hbm.1, f32[4,64]{1,0:T(4,128)} %bitcast.14, ...), custom_call_target="tpu_custom_call" | custom-call | tf_op jit(solution)/shard_map/pallas_call | solution.py:673
  26.3 0.6 %copy.11 = bf16[1,4,448]{2,1,0:T(4,128)(2,1)} copy(bf16[1,4,448]{2,1,0:T(4,128)(2,1)S(1)} %bitcast.8) | data formatting | bytes 7168

commit v9 on v8

--- a/solution.py
+++ b/solution.py
@@ -548,7 +548,6 @@
             remote(src_of(k), dst.at[k], send, recv(k), group, 2 * peers[k] + other).start()
 
     st = (lambda k: st_send, st_all, st_s, lambda k: st_r)
-    exchange(*st, far_first)
     probs = [each.astype(BF16) for each in probs]
     o = (lambda k: out_send.at[peers[k]], out_recv, o_s, lambda k: o_r.at[k // quarter])
     middle = quarter + quarter // 2
@@ -562,6 +561,8 @@
         )
         out_send[pl.ds(first, count)] = block_out.astype(BF16).reshape(count, wide, rows)
         exchange(*o, ks)
+        if ks[-1] == quarter:
+            exchange(*st, far_first)
 
     def turn(j):
         step = per * width

time: 27.1 us -> 27.1 us (level)
  no operation moved by 1% of the time
where the time goes in v9:
time: 27.1 us; the launch traced here: 27 us
  Pallas kernels  26.4 us (97%)
  local copies, waits for them, and re-layouts  0.6 us (2%)
    pallas_call x1, Pallas kernels, paired(): pl.pallas_call(functools.partial(pair_kernel, n, groups, heads, drafts),...  26.4 us
    unnamed x1, local copies, waits for them, and re-layouts  0.6 us

profile of v9, /device:TPU:0, one launch (start us, length us, event | category | flops | bytes accessed | tf_op | source)
XLA Modules:
  0.0 27.0 jit_solution(18067456667457060988)
XLA Ops:
  0.0 26.4 %shard_map.91 = bf16[4,448]{1,0:T(4,128)(2,1)S(1)} custom-call(bf16[4,64,128]{2,1,0:T(8,128)(2,1)} %bitcast.11, bf16[4,64,64]{2,1,0:T(8,128)(2,1)} %bitcast.12, bf16[512,512]{1,0:T(8,128)(2,1)} %bitcast.10, bf16[64,512]{1,0:T(8,128)(2,1)} %bitcast.13, bf16[64,32,128]{2,1,0:T(8,128)(2,1)} %kq_hbm.1, f32[4,64]{1,0:T(4,128)} %bitcast.14, ...), custom_call_target="tpu_custom_call" | custom-call | tf_op jit(solution)/shard_map/pallas_call | solution.py:674
  26.4 0.6 %copy.11 = bf16[1,4,448]{2,1,0:T(4,128)(2,1)} copy(bf16[1,4,448]{2,1,0:T(4,128)(2,1)S(1)} %bitcast.8) | data formatting | bytes 7168
